TPU v7x, 32 devices: a whole 2x2x4 slice. The times are simulated.
32 devices in a mesh: dp: 2 (over x), inner: 4 (over z), vocab: 4 (over y, core).
Axes of the slice: x: 2, y: 2, z: 4, core: 2. Of those that a mesh axis runs over, the one named last changes fastest.
Arguments:
- hidden: bfloat16 [1024, 1536], P('dp'), parts along dimension 0
- w_head: bfloat16 [1536, 151936], P(None, ('vocab', 'inner'))
- inv_temp: float32 [1024], P('dp'), parts along dimension 0
- target_id: int32 [1024], P('dp'), parts along dimension 0
Outputs:
- output 1: float32 [1024, 151936], P('dp', ('vocab', 'inner')), parts along dimension 0
- output 2: float32 [1024], P('dp'), parts along dimension 0
There are 2 independent parts. A program takes and returns all parts, laid end to end along the dimension named above; an argument that names none is the same for every part.
All inputs are finite; a program needn't handle non-finite values.
Results may differ from a plain program's by a relative error of at most 0.001.
Values are sent between devices in bfloat16 or wider.
A program may use at most 1 GiB of HBM per device.

v0:
```python
import jax
import jax.numpy as jnp
from jax import lax
from jax.sharding import PartitionSpec as P

VOCAB_AXES = ('vocab', 'inner')


def solution(mesh):
    inner_count = mesh.shape['inner']

    def local_step(hidden, w_shard, inv_temp, target_id):
        width = w_shard.shape[1]
        logits = jnp.dot(hidden, w_shard, preferred_element_type=jnp.float32) * inv_temp[:, None]
        local_max = jnp.max(logits, axis=1)
        exp_local = jnp.exp(logits - local_max[:, None])
        local_sum = jnp.sum(exp_local, axis=1)
        global_max = lax.pmax(local_max, VOCAB_AXES)
        max_factor = jnp.exp(local_max - global_max)
        global_sum = lax.psum(local_sum * max_factor, VOCAB_AXES)
        row_scale = max_factor / global_sum
        local_cdf = jnp.cumsum(exp_local, axis=1) * row_scale[:, None]
        shard_total = local_cdf[:, -1]
        inner_idx = lax.axis_index('inner')
        vocab_idx = lax.axis_index('vocab')
        inner_totals = lax.all_gather(shard_total, 'inner')
        inner_mask = jnp.arange(inner_totals.shape[0]) < inner_idx
        inner_before = jnp.sum(jnp.where(inner_mask[:, None], inner_totals, 0.0), axis=0)
        chip_totals = lax.all_gather(jnp.sum(inner_totals, axis=0), 'vocab')
        chip_mask = jnp.arange(chip_totals.shape[0]) < vocab_idx
        chip_before = jnp.sum(jnp.where(chip_mask[:, None], chip_totals, 0.0), axis=0)
        cdf_table = local_cdf + (chip_before + inner_before)[:, None]
        shard_start = (vocab_idx * inner_count + inner_idx) * width
        local_col = target_id - shard_start
        picked = jnp.sum(jnp.where(jnp.arange(width)[None, :] == local_col[:, None], cdf_table, 0.0), axis=1)
        cdf_target = lax.psum(picked, VOCAB_AXES)
        return cdf_table, cdf_target

    return jax.shard_map(local_step, mesh=mesh, in_specs=(P('dp', None), P(None, VOCAB_AXES), P('dp'), P('dp')), out_specs=(P('dp', VOCAB_AXES), P('dp')), check_vma=False)
```

profile of v0, /device:TPU:0, one launch (start us, length us, event | category | flops | bytes accessed | tf_op | source)
XLA Modules:
  0.0 261.0 jit_solution(12110259379194842419)
XLA Ops:
  0.6 0.0 copy-start
  0.6 0.0 copy-start.3
  0.7 1.4 copy-done
  2.0 23.2 %multiply_reduce_fusion = (f32[512]{0:T(512)S(1)}, f32[512,9496]{0,1:T(8,128)}) fusion(f32[512]{0:T(512)} %param.6, bf16[512,1536]{1,0:T(8,128)(2,1)S(1)} %copy-done, bf16[1536,9496]{0,1:T(8,128)(2,1)} %param.5), kind=kOutput, calls=%fused_computation.6 | convolution fusion | flops 14945640448 | bytes 50196480 | tf_op jit(solution)/shard_map/dot_general | solution.py:14
  25.2 0.0 copy-done.3
  25.2 16.0 %fusion.5 = (f32[512]{0:T(512)S(1)}, f32[512,9496]{0,1:T(8,128)}) fusion(f32[512]{0:T(512)S(1)} %get-tuple-element.8, f32[512,9496]{0,1:T(8,128)} %get-tuple-element.9, f32[512]{0:T(512)S(1)} %copy-done.3), kind=kLoop, calls=%fused_computation.19 | loop fusion | flops 14585344 | bytes 38901760 | tf_op jit(solution)/shard_map/reduce_sum | solution.py:17
  41.3 35.2 %pmax.7 = f32[512]{0:T(512)S(1)} all-reduce(f32[512]{0:T(512)S(1)} %get-tuple-element.8), channel_id=1, replica_groups=mesh['dp'=2,'inner'=4,'vocab'=4] {'vocab','inner'}, use_global_device_ids=true, to_apply=%region_3.0 | all-reduce | flops 512 | bytes 4096 | tf_op jit(solution)/shard_map/pmax | solution.py:18
  76.5 29.8 %psum.14 = f32[512]{0:T(512)S(1)} all-reduce(f32[512]{0:T(512)S(1)} %fusion.4), channel_id=1, replica_groups=mesh['dp'=2,'inner'=4,'vocab'=4] {'vocab','inner'}, use_global_device_ids=true, to_apply=%region_5.6 | all-reduce | flops 512 | bytes 4096 | tf_op jit(solution)/shard_map/psum | solution.py:20
  106.3 15.4 %pad.3 = f32[512,9600]{0,1:T(8,128)} pad(f32[512,9496]{0,1:T(8,128)} %get-tuple-element.7, f32[]{:T(128)} %constant.5.clone.1), padding=0_0x0_104 | pad | bytes 39108612 | tf_op jit(solution)/shard_map/pad
  121.7 21.1 %fusion = f32[512,75,128]{0,1,2:T(8,128)} fusion(f32[512,75,128]{0,2,1:T(8,128)} %bitcast.15), kind=kOutput, calls=%fused_computation | output fusion | flops 624230400 | bytes 39321600 | tf_op jit(solution)/shard_map/reduce-window
  142.8 0.9 slice_bitcast_fusion
  143.8 0.2 reduce-window.9
  143.9 17.3 %broadcast_add_fusion = f32[512,75,128]{0,1,2:T(8,128)} fusion(f32[512,75,128]{0,1,2:T(8,128)} %fusion, f32[512,75]{0,1:T(8,128)S(1)} %bitcast.16), kind=kLoop, calls=%fused_computation.7 | loop fusion | flops 4915200 | bytes 39475200 | tf_op jit(solution)/shard_map/reduce_window_sum
  161.3 17.7 %copy.10 = f32[512,75,128]{0,2,1:T(8,128)S(1)} copy(f32[512,75,128]{0,1,2:T(8,128)} %broadcast_add_fusion) | data formatting | bytes 39321600 | tf_op jit(solution)/shard_map/reduce_window_sum
  179.0 0.0 copy-start.2
  179.0 0.0 copy-start.4
  179.0 9.2 %slice_multiply_fusion = f32[512,9496]{0,1:T(8,128)} fusion(f32[512,9600]{0,1:T(8,128)S(1)} %bitcast.13, f32[512]{0:T(512)S(1)} %fusion.3), kind=kLoop, calls=%fused_computation.2 | loop fusion | flops 4861952 | bytes 38897664 | tf_op jit(solution)/shard_map/mul | solution.py:22
  188.2 3.3 %copy-done.2 = f32[512,75,128]{0,2,1:T(8,128)} copy-done((f32[512,75,128]{0,2,1:T(8,128)}, f32[512,75,128]{0,2,1:T(8,128)S(1)}, u32[]{:S(2)}) %copy-start.2) | copy-done | bytes 19660824
  191.5 0.7 slice.19
  192.2 13.0 %all-gather = f32[2048,1]{0,1:T(1,128)S(1)} all-gather(f32[512,1]{0,1:T(1,128)S(1)} %slice.19), channel_id=2, replica_groups=mesh['dp'=2,'inner'=4,'vocab'=4] {'inner'}, dimensions={0}, use_global_device_ids=true | all-gather | bytes 10240 | tf_op jit(solution)/shard_map/all_gather | solution.py:26
  205.3 0.5 broadcast.23
  205.8 0.7 reduce.3
  206.5 0.1 select_reduce_fusion.1
  206.6 5.2 %all-gather.2 = f32[4,1,512]{2,1,0:T(1,128)S(1)} all-gather(f32[1,1,512]{2,1,0:T(1,128)S(1)} %bitcast.17), channel_id=3, replica_groups=mesh['dp'=2,'inner'=4,'vocab'=4] {'vocab'}, dimensions={0}, use_global_device_ids=true | all-gather | bytes 10240 | tf_op jit(solution)/shard_map/all_gather | solution.py:29
  211.7 0.1 fusion.2
  211.8 0.0 copy-done.4
  211.9 0.0 copy-start.1
  211.9 16.8 %select_reduce_fusion = (f32[512]{0:T(512)S(1)}, f32[512,9496]{0,1:T(8,128)}) fusion(s32[512]{0:T(512)S(1)} %broadcast_subtract_fusion, f32[512]{0:T(512)S(1)} %add.24, f32[512]{0:T(512)S(1)} %fusion.3, f32[512,9600]{0,1:T(8,128)} %bitcast.14), kind=kLoop, calls=%fused_computation.3 | loop fusion | flops 24309248 | bytes 38903808 | tf_op jit(solution)/shard_map/reduce_sum | solution.py:35
  228.6 32.4 %psum.15 = f32[512]{0:T(512)} all-reduce(f32[512]{0:T(512)S(1)} %get-tuple-element.4), channel_id=1, replica_groups=mesh['dp'=2,'inner'=4,'vocab'=4] {'vocab','inner'}, use_global_device_ids=true, to_apply=%region_10.11 | all-reduce | flops 512 | bytes 4096 | tf_op jit(solution)/shard_map/psum | solution.py:36
  261.0 0.0 copy-done.1
  (7 shorter events, 0.1 us)
Async XLA Ops:
  0.6 1.4 copy-start
  0.6 24.6 %copy-start.3 = (f32[512]{0:T(512)S(1)}, f32[512]{0:T(512)}, u32[]{:S(2)}) copy-start(f32[512]{0:T(512)} %param.6) | copy-start | bytes 6148
  179.0 12.5 %copy-start.2 = (f32[512,75,128]{0,2,1:T(8,128)}, f32[512,75,128]{0,2,1:T(8,128)S(1)}, u32[]{:S(2)}) copy-start(f32[512,75,128]{0,2,1:T(8,128)S(1)} %copy.10) | copy-start | bytes 58982404
  179.0 32.8 %copy-start.4 = (s32[512]{0:T(512)S(1)}, s32[512]{0:T(512)}, u32[]{:S(2)}) copy-start(s32[512]{0:T(512)} %param.7) | copy-start | bytes 6148
  211.9 49.2 %copy-start.1 = (bf16[512,1536]{1,0:T(8,128)(2,1)S(1)}, bf16[512,1536]{1,0:T(8,128)(2,1)}, u32[]{:S(2)}) copy-start(bf16[512,1536]{1,0:T(8,128)(2,1)} %param.4) | copy-start | bytes 4718596
where the time goes:
time: 262 us; the launch traced here: 261 us
  blocking collectives  116 us (44%)
  other arithmetic  81.5 us (31%)
  local copies, waits for them, and re-layouts  40 us (15%)
  matrix products  23.2 us (9%)
    another operation x3, other arithmetic  38.6 us
    pmax x1, blocking collectives, local_step(): global_max = lax.pmax(local_max, VOCAB_AXES)  35.2 us
    psum x1, blocking collectives, local_step(): cdf_target = lax.psum(picked, VOCAB_AXES)  32.4 us
    psum x1, blocking collectives, local_step(): global_sum = lax.psum(local_sum * max_factor, VOCAB_AXES)  29.8 us
    dot_general x1, matrix products, local_step(): jnp.dot(hidden, w_shard, preferred_element_type=jnp.float32)  23.2 us
    another operation x2, local copies, waits for them, and re-layouts  18.7 us
    reduce_sum x1, other arithmetic, local_step(): jnp.sum(jnp.where(jnp.arange(width)[None, :] == local_col[:, None], cdf_t...  16.8 us
    reduce_sum x1, other arithmetic, local_step(): local_sum = jnp.sum(exp_local, axis=1)  16 us

commit v1 on v0

v1 whole, which is shorter than its diff:
```python
import functools

import jax
import jax.numpy as jnp
from jax import lax
from jax.experimental import pallas as pl
from jax.experimental.pallas import tpu as pltpu
from jax.sharding import PartitionSpec as P

VOCAB_AXES = ('vocab', 'inner')
F32 = jnp.float32
LANES = 128
ROWS = 432
W_SLOTS = 4
OUT_SLOTS = 3


def _row(block, k):
    return block[k:k + 1, :]


def _head_kernel(n_vocab, n_inner, invt_hbm, tgt_hbm, hid_hbm, w_hbm, c_ref, off_ref, fac_ref, pre_ref, glob_ref,
                 invt_ref, tgt_ref, hid, hid_t, wbuf, z, mx, tot, tq, recv, hsem, wsem, send_sem, recv_sem):
    vocab, depth = w_hbm.shape
    batch = hid.shape[0]
    n_l = batch // LANES
    n_t = pl.cdiv(vocab, ROWS)
    last_rows = vocab - (n_t - 1) * ROWS
    n_dev = n_vocab * n_inner
    my_v, my_i = lax.axis_index('vocab'), lax.axis_index('inner')
    me = my_v * n_inner + my_i
    shard_start = me * vocab

    def peer(k):
        p = lax.rem(me + k, n_dev)
        return p, {'vocab': p // n_inner, 'inner': lax.rem(p, n_inner)}

    barrier = pltpu.get_barrier_semaphore()
    for k in range(1, n_dev):
        pl.semaphore_signal(barrier, inc=1, device_id=peer(k)[1], device_id_type=pl.DeviceIdType.MESH)

    def w_copy(t, slot, rows):
        return pltpu.make_async_copy(
            w_hbm.at[pl.ds(t * ROWS, rows), :], wbuf.at[slot, pl.ds(0, rows), :], wsem.at[slot])

    small = [pltpu.make_async_copy(src, dst, hsem.at[k]) for k, (src, dst) in enumerate(
        [(hid_hbm, hid), (invt_hbm, invt_ref), (tgt_hbm, tgt_ref)])]
    for copy in small:
        copy.start()
    for t in range(W_SLOTS - 1):
        w_copy(t, t, ROWS).start()
    for copy in small:
        copy.wait()
    hid_t[...] = hid[...].T

    invt = [_row(invt_ref[...], l) for l in range(n_l)]
    sub = lax.broadcasted_iota(jnp.int32, (8, LANES), 0)

    def matmul(t, slot, zslot, rows):
        zt = jnp.dot(wbuf[slot, :rows, :], hid_t[...], preferred_element_type=F32)
        for l in range(n_l):
            zl = zt[:, l * LANES:(l + 1) * LANES] * invt[l]
            z[zslot, l, :rows, :] = zl
            mx[t, l:l + 1, :] = jnp.max(zl, axis=0, keepdims=True)

    def prefix(t, zslot, rows):
        group = rows // 8
        first = shard_start + t * ROWS
        peak = [jnp.broadcast_to(mx[t, l:l + 1, :], (8, LANES)) for l in range(n_l)]
        rel = [tgt_ref[l:l + 1, :] - first - sub * group for l in range(n_l)]
        acc = [jnp.zeros((8, LANES), F32) for _ in range(n_l)]
        at_target = [jnp.zeros((8, LANES), F32) for _ in range(n_l)]
        for j in range(group):
            for l in range(n_l):
                e = jnp.exp(z.at[zslot, l][pl.ds(j, 8, stride=group), :] - peak[l])
                acc[l] = acc[l] + e
                c_ref[pl.ds(t * ROWS + 8 * j, 8), l * LANES:(l + 1) * LANES] = acc[l]
                at_target[l] = jnp.where(rel[l] == j, acc[l], at_target[l])
        for l in range(n_l):
            x = acc[l]
            for s in (1, 2, 4):
                x = x + jnp.where(sub >= s, pltpu.roll(x, s, 0), 0.0)
            excl = jnp.where(sub >= 1, pltpu.roll(x, 1, 0), 0.0)
            off_ref[t, l * 8:(l + 1) * 8, :] = excl
            tot[t, l:l + 1, :] = x[7:8, :]
            inside = (rel[l] >= 0) & (rel[l] < group)
            tq[t, l:l + 1, :] = jnp.sum(jnp.where(inside, at_target[l] + excl, 0.0), axis=0, keepdims=True)

    w_copy(0, 0, ROWS).wait()
    w_copy(W_SLOTS - 1, W_SLOTS - 1, ROWS).start()
    matmul(0, 0, 0, ROWS)

    def step(t, _):
        slot = lax.rem(t, W_SLOTS)
        w_copy(t, slot, ROWS).wait()
        ahead = t + W_SLOTS - 1
        ahead_slot = lax.rem(ahead, W_SLOTS)

        @pl.when(ahead < n_t - 1)
        def _():
            w_copy(ahead, ahead_slot, ROWS).start()

        @pl.when(ahead == n_t - 1)
        def _():
            w_copy(n_t - 1, ahead_slot, last_rows).start()

        zslot = lax.rem(t, 2)
        matmul(t, slot, zslot, ROWS)
        prefix(t - 1, 1 - zslot, ROWS)
        return 0

    lax.fori_loop(1, n_t - 1, step, 0)
    t_last = n_t - 1
    w_copy(t_last, t_last % W_SLOTS, last_rows).wait()
    matmul(t_last, t_last % W_SLOTS, t_last % 2, last_rows)
    prefix(t_last - 1, (t_last - 1) % 2, ROWS)
    prefix(t_last, t_last % 2, last_rows)

    tgt = tgt_ref[...]
    m_loc = jnp.max(mx[...], axis=0)
    run = jnp.zeros((n_l, LANES), F32)
    q_loc = jnp.zeros((n_l, LANES), F32)
    for t in range(n_t):
        fac = jnp.exp(mx[t] - m_loc)
        fac_ref[t] = fac
        pre_ref[t] = run
        lo = shard_start + t * ROWS
        hi = shard_start + min((t + 1) * ROWS, vocab)
        q_loc = q_loc + jnp.where((tgt >= lo) & (tgt < hi), tq[t] * fac + run, 0.0)
        run = run + tot[t] * fac
    recv[me, 0:n_l, :] = m_loc
    recv[me, n_l:2 * n_l, :] = run
    recv[me, 2 * n_l:3 * n_l, :] = q_loc

    pl.semaphore_wait(barrier, n_dev - 1)

    def stat_copy(k):
        return pltpu.make_async_remote_copy(
            src_ref=recv.at[me], dst_ref=recv.at[me], send_sem=send_sem.at[k], recv_sem=recv_sem.at[me],
            device_id=peer(k)[1], device_id_type=pl.DeviceIdType.MESH)

    for k in range(1, n_dev):
        stat_copy(k).start()
    for k in range(1, n_dev):
        p, where = peer(k)
        pltpu.make_async_remote_copy(
            src_ref=recv.at[p], dst_ref=recv.at[p], send_sem=send_sem.at[k], recv_sem=recv_sem.at[p],
            device_id=where, device_id_type=pl.DeviceIdType.MESH).wait_recv()

    m_all = recv[0, 0:n_l, :]
    for p in range(1, n_dev):
        m_all = jnp.maximum(m_all, recv[p, 0:n_l, :])
    total = jnp.zeros((n_l, LANES), F32)
    before = jnp.zeros((n_l, LANES), F32)
    up_to = jnp.zeros((n_l, LANES), F32)
    for p in range(n_dev):
        f = jnp.exp(recv[p, 0:n_l, :] - m_all)
        s = recv[p, n_l:2 * n_l, :] * f
        total = total + s
        before = before + jnp.where(p < me, s, 0.0)
        up_to = up_to + jnp.where(tgt >= (p + 1) * vocab, s, recv[p, 2 * n_l:3 * n_l, :] * f)
    glob_ref[0] = jnp.exp(m_loc - m_all) / total
    glob_ref[1] = before / total
    glob_ref[2] = up_to / total
    for k in range(1, n_dev):
        stat_copy(k).wait_send()


def _write_kernel(c_ref, off_ref, fac_ref, pre_ref, glob_ref, out_hbm, tgt_out, stage, sem):
    vocab, batch = out_hbm.shape
    n_l = batch // LANES
    n_t = pl.cdiv(vocab, ROWS)
    last_rows = vocab - (n_t - 1) * ROWS
    gain = glob_ref[0]
    base = glob_ref[1]
    tgt_out[...] = glob_ref[2]

    def out_copies(t, slot, rows):
        return [pltpu.make_async_copy(
            stage.at[slot, l, pl.ds(0, rows), :],
            out_hbm.at[pl.ds(t * ROWS, rows), l * LANES:(l + 1) * LANES], sem.at[slot, l]) for l in range(n_l)]

    def fill(t, slot, rows):
        group = rows // 8
        a_all = fac_ref[t] * gain
        d_all = pre_ref[t] * gain + base
        for l in range(n_l):
            a = jnp.broadcast_to(_row(a_all, l), (8, LANES))
            b = off_ref[t, l * 8:(l + 1) * 8, :] * a + _row(d_all, l)
            for j in range(group):
                c = c_ref[pl.ds(t * ROWS + 8 * j, 8), l * LANES:(l + 1) * LANES]
                stage.at[slot, l][pl.ds(j, 8, stride=group), :] = c * a + b

    def step(t, _):
        slot = lax.rem(t, OUT_SLOTS)

        @pl.when(t >= OUT_SLOTS)
        def _():
            for copy in out_copies(t - OUT_SLOTS, slot, ROWS):
                copy.wait()

        fill(t, slot, ROWS)
        for copy in out_copies(t, slot, ROWS):
            copy.start()
        return 0

    lax.fori_loop(0, n_t - 1, step, 0)
    t_last = n_t - 1
    for copy in out_copies(t_last - OUT_SLOTS, t_last % OUT_SLOTS, ROWS):
        copy.wait()
    fill(t_last, t_last % OUT_SLOTS, last_rows)
    for copy in out_copies(t_last, t_last % OUT_SLOTS, last_rows):
        copy.start()
    for t in range(n_t - OUT_SLOTS, n_t):
        for copy in out_copies(t, t % OUT_SLOTS, last_rows if t == t_last else ROWS):
            copy.wait()


def solution(mesh):
    n_vocab, n_inner = mesh.shape['vocab'], mesh.shape['inner']
    n_dev = n_vocab * n_inner
    vmem = pl.BlockSpec(memory_space=pltpu.VMEM)
    hbm = pl.BlockSpec(memory_space=pltpu.HBM)

    def local_step(hidden, w_shard, inv_temp, target_id):
        batch, depth = hidden.shape
        vocab = w_shard.shape[1]
        n_l = batch // LANES
        n_t = pl.cdiv(vocab, ROWS)
        mid_shapes = [(vocab, batch), (n_t, 8 * n_l, LANES), (n_t, n_l, LANES), (n_t, n_l, LANES), (3, n_l, LANES)]
        mids = pl.pallas_call(
            functools.partial(_head_kernel, n_vocab, n_inner),
            out_shape=[pltpu.VMEM(s, F32) for s in mid_shapes],
            in_specs=[hbm] * 4,
            out_specs=[vmem] * 5,
            scratch_shapes=[
                pltpu.VMEM((n_l, LANES), F32),
                pltpu.VMEM((n_l, LANES), jnp.int32),
                pltpu.VMEM((batch, depth), jnp.bfloat16),
                pltpu.VMEM((depth, batch), jnp.bfloat16),
                pltpu.VMEM((W_SLOTS, ROWS, depth), jnp.bfloat16),
                pltpu.VMEM((2, n_l, ROWS, LANES), F32),
                pltpu.VMEM((n_t, n_l, LANES), F32),
                pltpu.VMEM((n_t, n_l, LANES), F32),
                pltpu.VMEM((n_t, n_l, LANES), F32),
                pltpu.VMEM((n_dev, 3 * n_l, LANES), F32),
                pltpu.SemaphoreType.DMA((3,)),
                pltpu.SemaphoreType.DMA((W_SLOTS,)),
                pltpu.SemaphoreType.DMA((n_dev,)),
                pltpu.SemaphoreType.DMA((n_dev,)),
            ],
            compiler_params=pltpu.CompilerParams(
                collective_id=0, has_side_effects=True, vmem_limit_bytes=24 * 2 ** 20),
            name='head',
        )(inv_temp.reshape(n_l, LANES), target_id.reshape(n_l, LANES), hidden, w_shard.T)
        table_t, at_target = pl.pallas_call(
            _write_kernel,
            out_shape=[jax.ShapeDtypeStruct((vocab, batch), F32), jax.ShapeDtypeStruct((n_l, LANES), F32)],
            in_specs=[vmem] * 5,
            out_specs=[hbm, vmem],
            scratch_shapes=[
                pltpu.VMEM((OUT_SLOTS, n_l, ROWS, LANES), F32),
                pltpu.SemaphoreType.DMA((OUT_SLOTS, n_l)),
            ],
            compiler_params=pltpu.CompilerParams(vmem_limit_bytes=8 * 2 ** 20),
            name='table',
        )(*mids)
        return table_t.T, at_target.reshape(batch)

    return jax.shard_map(local_step, mesh=mesh, in_specs=(P('dp', None), P(None, VOCAB_AXES), P('dp'), P('dp')),
                         out_specs=(P('dp', VOCAB_AXES), P('dp')), check_vma=False)
```

time: 262 us -> 44.9 us (0.17)
  blocking collectives: 116 us -> 0 us
  other arithmetic: 81.5 us -> 0 us
  Pallas kernels: 0 us -> 41.3 us
  local copies, waits for them, and re-layouts: 40 us -> 2.76 us
  matrix products: 23.2 us -> 0 us
    psum x2 -> x0, blocking collectives: 62.2 us -> none  [the longest x1 32.4 us: local_step(): cdf_target = lax.psum(picked, VOCAB_AXES)]
    pallas_call x0 -> x2, Pallas kernels: none -> 41.3 us  [the longest x1 32.9 us: local_step(): pl.pallas_call(functools.partial(_head_kernel, n_vocab, n_inner), out_sha...]
    another operation x3 -> x0, other arithmetic: 38.6 us -> none
    pmax x1 -> x0, blocking collectives: 35.2 us -> none  [local_step(): global_max = lax.pmax(local_max, VOCAB_AXES)]
    reduce_sum x4 -> x0, other arithmetic: 33 us -> none  [the longest x1 16.8 us: local_step(): jnp.sum(jnp.where(jnp.arange(width)[None, :] == local_col[:, None], cdf_t...]
    dot_general x1 -> x0, matrix products: 23.2 us -> none  [local_step(): jnp.dot(hidden, w_shard, preferred_element_type=jnp.float32)]
    another operation x2 -> x0, local copies, waits for them, and re-layouts: 18.7 us -> none
    all_gather x2 -> x0, blocking collectives: 18.2 us -> none  [the longest x1 13 us: local_step(): inner_totals = lax.all_gather(shard_total, 'inner')]
where the time goes in v1:
time: 44.9 us; the launch traced here: 44.7 us
  Pallas kernels  41.3 us (92%)
  local copies, waits for them, and re-layouts  2.76 us (6%)
  between operations  0.65 us (1%)
    pallas_call x1, Pallas kernels, local_step(): pl.pallas_call(functools.partial(_head_kernel, n_vocab, n_inner), out_sha...  32.9 us
    pallas_call x1, Pallas kernels, local_step(): pl.pallas_call(_write_kernel, out_shape=[jax.ShapeDtypeStruct((vocab, bat...  8.42 us
    unnamed x6, local copies, waits for them, and re-layouts  2.76 us

profile of v1, /device:TPU:0, one launch (start us, length us, event | category | flops | bytes accessed | tf_op | source)
XLA Modules:
  0.0 44.7 jit_solution(1359774939286195863)
XLA Ops:
  0.6 0.0 copy-start
  0.6 1.4 %copy-done = bf16[512,1536]{1,0:T(8,128)(2,1)S(1)} copy-done((bf16[512,1536]{1,0:T(8,128)(2,1)S(1)}, bf16[512,1536]{1,0:T(8,128)(2,1)}, u32[]{:S(2)}) %copy-start) | copy-done | bytes 1572888
  2.0 0.0 copy-start.1
  2.0 0.7 %copy-done.1 = f32[512]{0:T(512)S(1)} copy-done((f32[512]{0:T(512)S(1)}, f32[512]{0:T(512)}, u32[]{:S(2)}) %copy-start.1) | copy-done | bytes 2072
  2.7 0.0 copy-start.2
  2.7 0.7 %copy-done.2 = s32[512]{0:T(512)S(1)} copy-done((s32[512]{0:T(512)S(1)}, s32[512]{0:T(512)}, u32[]{:S(2)}) %copy-start.2) | copy-done | bytes 2072
  3.4 32.9 %head.1 = (f32[9496,512]{1,0:T(8,128)S(1)}, f32[22,32,128]{2,1,0:T(8,128)S(1)}, f32[22,4,128]{2,1,0:T(4,128)S(1)}, f32[22,4,128]{2,1,0:T(4,128)S(1)}, f32[3,4,128]{2,1,0:T(4,128)S(1)}) custom-call(f32[4,128]{1,0:T(4,128)S(1)} %bitcast.5, s32[4,128]{1,0:T(4,128)S(1)} %bitcast.6, bf16[512,1536]{1,0:T(8,128)(2,1)S(1)} %copy-done, bf16[9496,1536]{1,0:T(8,128)(2,1)} %bitcast.7), custom_call_target="tpu_custom_call" | custom-call | tf_op jit(solution)/shard_map/head/pallas_call | solution.py:231
  36.3 8.4 %table.1 = (f32[9496,512]{1,0:T(8,128)}, f32[4,128]{1,0:T(4,128)}) custom-call(f32[9496,512]{1,0:T(8,128)S(1)} %get-tuple-element.9.c_ref, f32[22,32,128]{2,1,0:T(8,128)S(1)} %get-tuple-element.10.off_ref, f32[22,4,128]{2,1,0:T(4,128)S(1)} %get-tuple-element.11.fac_ref, f32[22,4,128]{2,1,0:T(4,128)S(1)} %get-tuple-element.12.pre_ref, ...), custom_call_target="tpu_custom_call" | custom-call | tf_op jit(solution)/shard_map/table/pallas_call | solution.py:256
Async XLA Ops:
  0.6 1.4 %copy-start = (bf16[512,1536]{1,0:T(8,128)(2,1)S(1)}, bf16[512,1536]{1,0:T(8,128)(2,1)}, u32[]{:S(2)}) copy-start(bf16[512,1536]{1,0:T(8,128)(2,1)} %hid_hbm.1) | copy-start | bytes 4718596
  2.0 0.7 %copy-start.1 = (f32[512]{0:T(512)S(1)}, f32[512]{0:T(512)}, u32[]{:S(2)}) copy-start(f32[512]{0:T(512)} %param.6) | copy-start | bytes 6148
  2.7 0.7 %copy-start.2 = (s32[512]{0:T(512)S(1)}, s32[512]{0:T(512)}, u32[]{:S(2)}) copy-start(s32[512]{0:T(512)} %param.7) | copy-start | bytes 6148
